TPU v7x, 32 devices: a whole 2x2x4 slice. The times are simulated.
32 devices in a mesh: subj: 16 (over z, y, x), vox: 2 (over core).
Axes of the slice: x: 2, y: 2, z: 4, core: 2. Of those that a mesh axis runs over, the one named last changes fastest.
Arguments:
- bold_series: float32 [16, 300, 16384], P('subj', None, 'vox')
- seed_index: int32 [256], replicated, may hold values from 0 to 16383
Outputs:
- group_z: float32 [16384, 256], P(('vox', 'subj'))
All inputs are finite; a program needn't handle non-finite values.
Results may differ from a plain program's by a relative error of at most 0.00031.
Values may be sent and summed in bfloat16 or wider, within the bound.
A program may use at most 64 MiB of HBM per device.

v0:
```python
import jax
import jax.numpy as jnp
from jax import lax
from jax.sharding import PartitionSpec as P

clip_limit = 0.99
epsilon = 1e-05


def normalize(series):
    demean_series = series - jnp.mean(series, axis=0, keepdims=True)
    spread = jnp.mean(demean_series * demean_series, axis=0, keepdims=True)
    return (demean_series * lax.rsqrt(spread + epsilon)).astype(jnp.bfloat16)


def arctanh_transform(cross_product, length):
    clipped = jnp.clip(cross_product * (1.0 / length), -clip_limit, clip_limit)
    return 0.5 * jnp.log((1.0 + clipped) / (1.0 - clipped))


def correlate(normed, seed_panel):
    return lax.dot_general(
        normed, seed_panel, (((0,), (0,)), ((), ())), preferred_element_type=jnp.float32
    )


def body(bold_series, seed_index):
    length = bold_series.shape[1]
    normed = normalize(bold_series[0])
    columns = normed.shape[1]
    groups = lax.axis_size("subj")
    anchor = lax.axis_index("vox") * columns
    offsets = seed_index - anchor
    inside = (offsets >= 0) & (offsets < columns)
    picked = jnp.take(normed, jnp.clip(offsets, 0, columns - 1), axis=1)
    masked = jnp.where(
        inside[None, :], picked.astype(jnp.float32), jnp.zeros(picked.shape, jnp.float32)
    )
    seed_panel = lax.psum(masked.astype(jnp.bfloat16), "vox")
    summed = lax.psum_scatter(
        arctanh_transform(correlate(normed, seed_panel), length),
        "subj",
        scatter_dimension=0,
        tiled=True,
    )
    return summed * (1.0 / groups)


def solution(mesh):
    in_specs = (P("subj", None, "vox"), P())
    out_specs = P(("vox", "subj"), None)
    return jax.shard_map(body, mesh=mesh, in_specs=in_specs, out_specs=out_specs, check_vma=False)
```

profile of v0, /device:TPU:10, one launch (start us, length us, event | category | flops | bytes accessed | tf_op | source)
XLA Modules:
  0.0 275.5 jit_solution(376455926714964036)
XLA Ops:
  6.5 0.0 all-reduce.2.cloned.1.call-start
  6.5 22.2 %copy.3 = f32[1,300,8192]{1,2,0:T(8,128)} copy(f32[1,300,8192]{2,0,1:T(1,128)} %param.2) | data formatting | bytes 19660800 | tf_op args[0]
  28.7 8.8 %reduce_sum.18 = f32[8192]{0:T(1024)S(1)} reduce(f32[1,300,8192]{2,0,1:T(1,128)} %param.2, f32[]{:T(128)} %constant.14.clone.1), dimensions={0,1}, to_apply=%region_0.0 | reduce | flops 2449408 | bytes 9863172 | tf_op jit(solution)/shard_map/reduce_sum | solution.py:11
  37.6 0.0 copy-start
  37.6 7.0 %multiply_reduce_fusion = f32[8192]{0:T(1024)S(1)} fusion(f32[1,300,8192]{1,2,0:T(8,128)} %copy.3, f32[8192]{0:T(1024)S(1)} %broadcast_multiply_fusion.1), kind=kLoop, calls=%fused_computation.3 | loop fusion | flops 7364608 | bytes 9895936 | tf_op jit(solution)/shard_map/reduce_sum | solution.py:12
  44.6 1.2 copy-done
  45.8 0.0 copy-start.1
  45.9 4.2 %multiply_convert_fusion = bf16[300,8192]{0,1:T(8,128)(2,1)} fusion(f32[1,300,8192]{1,2,0:T(8,128)S(1)} %copy-done, f32[8192]{0:T(1024)S(1)} %add_rsqrt_fusion, f32[8192]{0:T(1024)S(1)} %broadcast_multiply_fusion.1), kind=kLoop, calls=%fused_computation.2 | loop fusion | flops 7372800 | bytes 14811136 | tf_op jit(solution)/shard_map/convert_element_type | solution.py:13
  50.1 0.0 copy-done.1
  50.1 4.7 %gather_fusion = bf16[256,300]{1,0:T(8,128)(2,1)S(1)} fusion(bf16[300,8192]{0,1:T(8,128)(2,1)} %multiply_convert_fusion, s32[1024]{0:T(1024)S(1)} %pad_clamp_fusion), kind=kCustom, calls=%fused_computation | custom fusion | bytes 308224 | tf_op jit(solution)/shard_map/jit(_take)/gather | solution.py:35
  54.8 0.8 fusion.1
  55.7 0.0 all-reduce.2.cloned.1.call-update
  55.7 0.0 reduce-scatter.2.cloned.1.call-start
  55.7 19.6 %all-reduce.2.cloned.1.call-done = bf16[300,256]{0,1:T(8,128)(2,1)} async-done(((bf16[300,256]{0,1:T(8,128)(2,1)}), bf16[300,256]{0,1:T(8,128)(2,1)}) %all-reduce.2.cloned.1.call-update) | async-done | bytes 153616 | tf_op jit(solution)/shard_map/psum | solution.py:39
  75.3 9.3 %log_multiply_fusion = f32[8192,256]{1,0:T(8,128)} fusion(bf16[300,8192]{0,1:T(8,128)(2,1)} %multiply_convert_fusion, bf16[300,256]{0,1:T(8,128)(2,1)} %all-reduce.2.cloned.1.call-done), kind=kOutput, calls=%fused_computation.6 | convolution fusion | flops 1270874112 | bytes 13457408 | tf_op jit(solution)/shard_map/dot_general | solution.py:22
  84.7 0.0 reduce-scatter.2.cloned.1.call-update
  84.7 182.1 %reduce-scatter.2.cloned.1.call-done = f32[512,256]{1,0:T(8,128)} async-done(((f32[8192,256]{1,0:T(8,128)}), f32[512,256]{1,0:T(8,128)}) %reduce-scatter.2.cloned.1.call-update) | async-done | bytes 524304 | tf_op jit(solution)/shard_map/reduce_scatter | solution.py:40
  266.8 1.9 broadcast_multiply_fusion
  (4 shorter events, 0.0 us)
Async XLA Ops:
  6.5 68.8 %all-reduce.2.cloned.1.call-start = ((), (), s32[]{:S(2)}) async-start(), calls=%async_computation.1 | async-start | bytes 393216 | tf_op jit(solution)/shard_map/psum | solution.py:39
  37.6 8.3 %copy-start = (f32[1,300,8192]{1,2,0:T(8,128)S(1)}, f32[1,300,8192]{1,2,0:T(8,128)}, u32[]{:S(2)}) copy-start(f32[1,300,8192]{1,2,0:T(8,128)} %copy.3) | copy-start | bytes 29491204
  45.8 4.2 %copy-start.1 = (s32[256]{0:T(256)S(1)}, s32[256]{0:T(256)}, u32[]{:S(2)}) copy-start(s32[256]{0:T(256)} %param.3) | copy-start | bytes 3076
  55.7 211.1 %reduce-scatter.2.cloned.1.call-start = ((), (), s32[]{:S(2)}) async-start(), calls=%async_computation.2 | async-start | bytes 8912896 | tf_op jit(solution)/shard_map/reduce_scatter | solution.py:40
Sparse Core Ops, SparseCore 0:
  55.8 19.4 all-reduce.1
  84.8 181.9 reduce-scatter.1
where the time goes:
time: 276 us; the launch traced here: 275 us
  waiting for transfers between devices  202 us (73%)
  local copies, waits for them, and re-layouts  28.2 us (10%)
  other arithmetic  22.8 us (8%)
  between operations  13.5 us (5%)
  matrix products  9.32 us (3%)
    reduce_scatter x1, waiting for transfers between devices, body(): lax.psum_scatter(arctanh_transform(correlate(normed, seed_panel), length)...  182 us
    unnamed x5, local copies, waits for them, and re-layouts  23.4 us
    psum x1, waiting for transfers between devices, body(): seed_panel = lax.psum(masked.astype(jnp.bfloat16), 'vox')  19.6 us
    dot_general x1, matrix products, correlate(): lax.dot_general(normed, seed_panel, (((0,), (0,)), ((), ())), preferred_e...  9.32 us
    reduce_sum x1, other arithmetic, normalize(): demean_series = series - jnp.mean(series, axis=0, keepdims=True)  8.82 us
    reduce_sum x1, other arithmetic, normalize(): spread = jnp.mean(demean_series * demean_series, axis=0, keepdims=True)  6.99 us
  transfers between devices with their start and end apart: 2, of which 2 were waited for; matrix products, arithmetic and copies ran while one was open for 0% of the time, Pallas kernels for 0%

commit v1 on v0

--- a/solution.py
+++ b/solution.py
@@ -36,7 +36,7 @@
     masked = jnp.where(
         inside[None, :], picked.astype(jnp.float32), jnp.zeros(picked.shape, jnp.float32)
     )
-    seed_panel = lax.psum(masked.astype(jnp.bfloat16), "vox")
+    seed_panel = jnp.sum(lax.all_gather(masked.astype(jnp.bfloat16), "vox"), axis=0)
     summed = lax.psum_scatter(
         arctanh_transform(correlate(normed, seed_panel), length),
         "subj",

time: 276 us -> 258 us (0.935)
  waiting for transfers between devices: 202 us -> 182 us
    psum x1 -> x0, waiting for transfers between devices: 19.6 us -> none  [body(): seed_panel = lax.psum(masked.astype(jnp.bfloat16), 'vox')]
  transfers between devices with their start and end apart: 2 -> 1, of which waited for: 2 -> 1; matrix products, arithmetic and copies ran while one was open for 0% -> 0% of each run, Pallas kernels for 0% -> 0%
where the time goes in v1:
time: 258 us; the launch traced here: 257 us
  waiting for transfers between devices  182 us (71%)
  local copies, waits for them, and re-layouts  28.3 us (11%)
  other arithmetic  22 us (9%)
  between operations  13.5 us (5%)
  matrix products  9.1 us (4%)
    reduce_scatter x1, waiting for transfers between devices, body(): lax.psum_scatter(arctanh_transform(correlate(normed, seed_panel), length)...  182 us
    unnamed x5, local copies, waits for them, and re-layouts  23.4 us
    dot_general x1, matrix products, correlate(): lax.dot_general(normed, seed_panel, (((0,), (0,)), ((), ())), preferred_e...  9.1 us
    reduce_sum x1, other arithmetic, normalize(): demean_series = series - jnp.mean(series, axis=0, keepdims=True)  8.82 us
    reduce_sum x1, other arithmetic, normalize(): spread = jnp.mean(demean_series * demean_series, axis=0, keepdims=True)  6.99 us
  transfers between devices with their start and end apart: 1, of which 1 were waited for; matrix products, arithmetic and copies ran while one was open for 0% of the time, Pallas kernels for 0%

profile of v1, /device:TPU:10, one launch (start us, length us, event | category | flops | bytes accessed | tf_op | source)
XLA Modules:
  0.0 257.3 jit_solution(2154392798447492298)
XLA Ops:
  6.5 0.0 reduce-scatter.2.cloned.1.call-start
  6.5 22.2 %copy.7 = f32[1,300,8192]{1,2,0:T(8,128)} copy(f32[1,300,8192]{2,0,1:T(1,128)} %param.2) | data formatting | bytes 19660800 | tf_op args[0]
  28.7 8.8 %reduce_sum.30 = f32[8192]{0:T(1024)S(1)} reduce(f32[1,300,8192]{2,0,1:T(1,128)} %param.2, f32[]{:T(128)} %constant.15.clone.1), dimensions={0,1}, to_apply=%region_0.0 | reduce | flops 2449408 | bytes 9863172 | tf_op jit(solution)/shard_map/reduce_sum | solution.py:11
  37.6 0.0 copy-start
  37.6 7.0 %multiply_reduce_fusion = f32[8192]{0:T(1024)S(1)} fusion(f32[1,300,8192]{1,2,0:T(8,128)} %copy.7, f32[8192]{0:T(1024)S(1)} %broadcast_multiply_fusion.1), kind=kLoop, calls=%fused_computation.3 | loop fusion | flops 7364608 | bytes 9895936 | tf_op jit(solution)/shard_map/reduce_sum | solution.py:12
  44.6 1.2 copy-done
  45.8 0.0 copy-start.1
  45.9 4.2 %multiply_convert_fusion = bf16[300,8192]{0,1:T(8,128)(2,1)} fusion(f32[1,300,8192]{1,2,0:T(8,128)S(1)} %copy-done, f32[8192]{0:T(1024)S(1)} %add_rsqrt_fusion, f32[8192]{0:T(1024)S(1)} %broadcast_multiply_fusion.1), kind=kLoop, calls=%fused_computation.2 | loop fusion | flops 7372800 | bytes 14811136 | tf_op jit(solution)/shard_map/convert_element_type | solution.py:13
  50.1 0.0 copy-done.1
  50.1 4.7 %gather_fusion = bf16[256,300]{1,0:T(8,128)(2,1)S(1)} fusion(bf16[300,8192]{0,1:T(8,128)(2,1)} %multiply_convert_fusion, s32[1024]{0:T(1024)S(1)} %pad_clamp_fusion), kind=kCustom, calls=%fused_computation | custom fusion | bytes 308224 | tf_op jit(solution)/shard_map/jit(_take)/gather | solution.py:35
  54.8 0.1 copy.8
  55.0 2.0 all_gather.4
  57.1 0.1 reduce_sum.32
  57.1 9.1 %log_multiply_fusion = f32[8192,256]{1,0:T(8,128)} fusion(bf16[300,8192]{0,1:T(8,128)(2,1)} %multiply_convert_fusion, bf16[300,256]{1,0:T(8,128)(2,1)S(1)} %reduce_sum.32), kind=kOutput, calls=%fused_computation.6 | convolution fusion | flops 1270874112 | bytes 13457408 | tf_op jit(solution)/shard_map/dot_general | solution.py:22
  66.2 0.0 reduce-scatter.2.cloned.1.call-update
  66.2 182.3 %reduce-scatter.2.cloned.1.call-done = f32[512,256]{1,0:T(8,128)} async-done(((f32[8192,256]{1,0:T(8,128)}), f32[512,256]{1,0:T(8,128)}) %reduce-scatter.2.cloned.1.call-update) | async-done | bytes 524304 | tf_op jit(solution)/shard_map/reduce_scatter | solution.py:40
  248.5 1.9 broadcast_multiply_fusion
  (5 shorter events, 0.1 us)
Async XLA Ops:
  6.5 242.0 %reduce-scatter.2.cloned.1.call-start = ((), (), s32[]{:S(2)}) async-start(), calls=%async_computation.1 | async-start | bytes 8912896 | tf_op jit(solution)/shard_map/reduce_scatter | solution.py:40
  37.6 8.3 %copy-start = (f32[1,300,8192]{1,2,0:T(8,128)S(1)}, f32[1,300,8192]{1,2,0:T(8,128)}, u32[]{:S(2)}) copy-start(f32[1,300,8192]{1,2,0:T(8,128)} %copy.7) | copy-start | bytes 29491204
  45.8 4.2 %copy-start.1 = (s32[256]{0:T(256)S(1)}, s32[256]{0:T(256)}, u32[]{:S(2)}) copy-start(s32[256]{0:T(256)} %param.3) | copy-start | bytes 3076
Sparse Core Ops, SparseCore 0:
  66.4 182.1 reduce-scatter.1
